TPU v7x, 32 devices: a whole 2x2x4 slice. The times are simulated.
32 devices in a mesh: mem: 4 (over y, core), lat: 4 (over z), lon: 2 (over x).
Axes of the slice: x: 2, y: 2, z: 4, core: 2. Of those that a mesh axis runs over, the one named last changes fastest.
Arguments:
- fields: bfloat16 [4, 2, 96, 96, 512], P('mem', None, 'lat', 'lon'), may hold values from -6 to 6
- region: int32 [96, 96], P('lat', 'lon'), may hold values from 0 to 2
- gain_attn: float32 [512], replicated, may hold values from 0.1 to 1.9
- w_qkv: bfloat16 [512, 1536], P(None, ('mem', 'lat', 'lon')), may hold values from -1 to 1
- w_proj: bfloat16 [512, 512], P(None, ('mem', 'lat', 'lon')), may hold values from -0.25 to 0.25
- gain_mlp: float32 [512], replicated, may hold values from 0.1 to 1.9
- w_up: bfloat16 [512, 2048], P(None, ('mem', 'lat', 'lon')), may hold values from -0.25 to 0.25
- w_down: bfloat16 [2048, 512], P(None, ('mem', 'lat', 'lon')), may hold values from -0.125 to 0.125
Outputs:
- updated: bfloat16 [4, 2, 96, 96, 512], P('mem', None, 'lat', 'lon')
All inputs are finite; a program needn't handle non-finite values.
Results may differ from a plain program's by a relative error of at most 0.011.
Values may be sent and summed in bfloat16 or wider, within the bound.
A program may use at most 192 MiB of HBM per device.

v0:
```python
import functools

import jax
import jax.numpy as jnp
from jax import lax
from jax.experimental import pallas as pl
from jax.experimental.pallas import tpu as pltpu
from jax.sharding import PartitionSpec as P

HDIM = 32
WLAT = 6
WLON = 12
SH = 3
SL = 6
PAD = 8
LANES = 128
AXES = ("mem", "lat", "lon")
BIG = 1e9
EXP2_SCALE = 1.4426950408889634 / HDIM**0.5

eps = 1e-05

NT = (((1,), (1,)), ((), ()))
TN = (((0,), (0,)), ((), ()))
ALL = slice(None)


def dot32(a, b, dims):
    return lax.dot_general(a, b, dims, preferred_element_type=jnp.float32)


def norm(values, gain):
    average = jnp.mean(values, axis=-1, keepdims=True)
    centred = values - average
    variance = jnp.mean(centred * centred, axis=-1, keepdims=True)
    return (centred * lax.rsqrt(variance + eps) * gain).astype(jnp.bfloat16)


def window_order(bands, wins):
    edge = [(bands - 1, w) for w in range(wins)] + [(b, wins - 1) for b in range(bands - 1)]
    inner = [(b, w) for b in range(bands - 1) for w in range(wins - 1)]
    order = inner[:wins] + edge
    return order + inner[wins:], wins, len(order)


def gather_plan(dims):
    fine = [(d, "lon", "mem") if d % 2 == 0 else (d, "mem", "lon") for d in range(dims["lat"])]
    return [fine, [(None, "lon", "mem")], [(None, "lon", "mem")], [(None, "lon", "mem")]]


def gather_keys(dims):
    keys = []
    for i, parts in enumerate(gather_plan(dims)):
        keys += [("z", i, d) for d in range(1, dims["lat"])]
        for p, (_, a2, a3) in enumerate(parts):
            keys += [("c1", i, p)]
            keys += [(k, i, p, d) for d in range(1, dims[a2]) for k in ("s2", "c2")]
            keys += [(k, i, p, d) for d in range(1, dims[a3]) for k in ("s3", "c3")]
    return keys


HALO = ("rows", "cols", "corner", "id_rows", "id_cols", "id_corner", "back_rows", "back_cols", "back_corner")


class Links:
    def __init__(self, dims, weights, send_sem, recv_sem):
        self.dims = dims
        self.plan = gather_plan(dims)
        self.weights = weights
        self.send_sem = send_sem
        self.recv_sem = recv_sem
        self.slots = {key: n for n, key in enumerate(gather_keys(dims) + list(HALO))}
        mem = lax.axis_index("mem")
        self.core = lax.rem(mem, 2)
        self.at = {"mem": lax.div(mem, 2), "lat": lax.axis_index("lat"), "lon": lax.axis_index("lon")}
        self.partner = {"mem": self.at["mem"] * 2 + 1 - self.core}

    def moved(self, axis, d):
        return lax.rem(self.at[axis] + d + self.dims[axis], self.dims[axis])

    def device(self, **offsets):
        to = {}
        for axis, d in offsets.items():
            position = self.moved(axis, d)
            to[axis] = position * 2 + self.core if axis == "mem" else position
        return to

    def copy(self, key, src, dst, to):
        slot = self.slots[key]
        return pltpu.make_async_remote_copy(
            src_ref=src,
            dst_ref=dst,
            send_sem=self.send_sem.at[slot],
            recv_sem=self.recv_sem.at[slot],
            device_id=to,
            device_id_type=pl.DeviceIdType.MESH,
        )

    def block(self, i, **where):
        index = [where.get(axis, self.at[axis]) for axis in AXES]
        return self.weights[i].at[index[0], self.core, index[1], index[2]]

    def lat_of(self, i, p):
        d = self.plan[i][p][0]
        return ALL if d is None else self.moved("lat", -d)

    def first(self, i, d):
        block = self.block(i)
        return self.copy(("z", i, d), block, block, self.device(lat=d))

    def second(self, i, p, d):
        block = self.block(i, lat=self.lat_of(i, p))
        return self.copy(("s2", i, p, d), block, block, self.device(**{self.plan[i][p][1]: d}))

    def third(self, i, p, d):
        block = self.block(i, lat=self.lat_of(i, p), **{self.plan[i][p][1]: ALL})
        return self.copy(("s3", i, p, d), block, block, self.device(**{self.plan[i][p][2]: d}))

    def cross(self, stage, i, p, d=None):
        _, a2, a3 = self.plan[i][p]
        where = {"lat": self.lat_of(i, p)}
        if stage == 2:
            where[a2] = self.moved(a2, -d)
        if stage == 3:
            where[a2] = ALL
            where[a3] = self.moved(a3, -d)
        block = self.block(i, **where)
        key = ("c1", i, p) if stage == 1 else ("c%d" % stage, i, p, d)
        return self.copy(key, block, block, self.partner)

    def peers(self, axis):
        return range(1, self.dims[axis])

    def start_first(self, i):
        for d in self.peers("lat"):
            self.first(i, d).start()

    def to_second(self, i, p):
        lat, a2, _ = self.plan[i][p]
        for d in self.peers("lat"):
            if lat in (None, d):
                self.first(i, d).wait_recv()
        for d in self.peers(a2):
            self.second(i, p, d).start()
        self.cross(1, i, p).start()

    def to_third(self, i, p):
        _, a2, a3 = self.plan[i][p]
        for d in self.peers(a2):
            self.second(i, p, d).wait_recv()
        for d in self.peers(a3):
            self.third(i, p, d).start()
        for d in self.peers(a2):
            self.cross(2, i, p, d).start()

    def to_cross(self, i, p):
        for d in self.peers(self.plan[i][p][2]):
            self.third(i, p, d).wait_recv()
            self.cross(3, i, p, d).start()

    def crossings(self, i, p):
        _, a2, a3 = self.plan[i][p]
        yield self.cross(1, i, p)
        for d in self.peers(a2):
            yield self.cross(2, i, p, d)
        for d in self.peers(a3):
            yield self.cross(3, i, p, d)

    def arrive(self, i):
        for p in range(len(self.plan[i])):
            for copy in self.crossings(i, p):
                copy.wait_recv()

    def drain(self, i):
        for d in self.peers("lat"):
            self.first(i, d).wait_send()
        for p, (_, a2, a3) in enumerate(self.plan[i]):
            for d in self.peers(a2):
                self.second(i, p, d).wait_send()
            for d in self.peers(a3):
                self.third(i, p, d).wait_send()
            for copy in self.crossings(i, p):
                copy.wait_send()

    def greet(self):
        barrier = pltpu.get_barrier_semaphore()
        others = [self.partner]
        for axis in AXES:
            others += [self.device(**{axis: d}) for d in self.peers(axis)]
        others += [self.device(lat=1, lon=1), self.device(lat=-1, lon=-1)]
        for to in others:
            pl.semaphore_signal(barrier, inc=1, device_id=to, device_id_type=pl.DeviceIdType.MESH)
        pl.semaphore_wait(barrier, len(others))


def attention_kernel(
    dims,
    x_ref,
    hot_ref,
    gain_ref,
    wqkv_ref,
    wproj_ref,
    wup_ref,
    wdown_ref,
    resid_ref,
    cols_ref,
    up_ref,
    down_ref,
    ext_s,
    hotx_s,
    grid_s,
    hotg_s,
    tok_s,
    hot_s,
    normed_s,
    qkv_s,
    mix_s,
    wqkv_s,
    wproj_s,
    own_sem,
    send_sem,
    recv_sem,
):
    levels, clat, clon, width = x_ref.shape
    bands, wins = clat // WLAT, clon // WLON
    wtok = levels * WLAT * WLON
    order, early, late = window_order(bands, wins)
    count = len(order)
    groups = count // wins
    gtok = wins * wtok

    links = Links(dims, [wqkv_s, wproj_s, up_ref, down_ref], send_sem, recv_sem)
    own = [
        pltpu.make_async_copy(shard, links.block(i), own_sem.at[i])
        for i, shard in enumerate([wqkv_ref, wproj_ref, wup_ref, wdown_ref])
    ]
    own.append(pltpu.make_async_copy(x_ref, ext_s.at[:, pl.ds(0, clat), pl.ds(0, clon)], own_sem.at[4]))
    own.append(pltpu.make_async_copy(hot_ref, hotx_s.at[pl.ds(0, clat), pl.ds(0, clon)], own_sem.at[5]))
    for copy in own:
        copy.start()

    top, side = pl.ds(0, SH), pl.ds(0, PAD)
    body_rows, body_cols = pl.ds(0, clat), pl.ds(0, clon)
    below, beyond = pl.ds(clat, SH), pl.ds(clon, PAD)
    lat_prev, lon_prev, prev = links.device(lat=-1), links.device(lon=-1), links.device(lat=-1, lon=-1)
    rows_in = [
        links.copy("rows", x_ref.at[:, top], ext_s.at[:, below, body_cols], lat_prev),
        links.copy("id_rows", hot_ref.at[top], hotx_s.at[below, body_cols], lat_prev),
    ]
    cols_in = [
        links.copy("cols", x_ref.at[:, :, side], ext_s.at[:, body_rows, beyond], lon_prev),
        links.copy("id_cols", hot_ref.at[:, side], hotx_s.at[body_rows, beyond], lon_prev),
        links.copy("corner", x_ref.at[:, top, side], ext_s.at[:, below, beyond], prev),
        links.copy("id_corner", hot_ref.at[top, side], hotx_s.at[below, beyond], prev),
    ]

    links.greet()
    own[0].wait()
    links.start_first(0)
    links.to_second(0, 0)
    for copy in rows_in:
        copy.start()
    for i in range(1, 4):
        own[i].wait()
        links.start_first(i)
    for copy in own[4:]:
        copy.wait()

    def widen(rows, cols):
        def row(r, _):
            for l in range(levels):
                grid_s[l, r, cols, :] = ext_s[l, r, cols, :].astype(jnp.float32)
            hotg_s[r, cols, :] = hotx_s[r, cols, :].astype(jnp.float32)
            return 0

        lax.fori_loop(rows[0], rows[1], row, 0)

    def fetch(slot):
        b, w = order[slot]
        for r in range(WLAT):
            cols = pl.ds(SL + w * WLON, WLON)
            for l in range(levels):
                to = pl.ds(slot * wtok + (l * WLAT + r) * WLON, WLON)
                tok_s[to, :] = grid_s[l, SH + b * WLAT + r, cols, :]
                hot_s[to, :] = hotg_s[SH + b * WLAT + r, cols, :]

    def norms(first, last):
        def one(s, _):
            rows = pl.ds(pl.multiple_of(s * wtok, wtok), wtok)
            normed_s[rows, :] = norm(tok_s[rows, :], gain_ref[...])
            return 0

        lax.fori_loop(first, last, one, 0)

    fine = len(links.plan[0])
    widen((0, clat), pl.ds(0, clon))
    for p in range(1, fine):
        links.to_second(0, p)
    links.to_third(0, 0)
    for copy in cols_in:
        copy.start()
    for slot in list(range(early)) + list(range(late, count)):
        fetch(slot)
    for p in range(1, fine):
        links.to_third(0, p)
    norms(0, early)
    norms(late, count)
    for p in range(fine):
        links.to_cross(0, p)
    links.to_second(1, 0)
    for copy in rows_in + cols_in:
        copy.wait_recv()
    widen((0, clat), pl.ds(clon, PAD))
    widen((clat, clat + SH), pl.ds(0, clon + PAD))
    for slot in range(early, late):
        fetch(slot)
    norms(early, late)
    links.arrive(0)

    wqkv = wqkv_s[...].reshape(3 * width, width)
    per = LANES // HDIM
    lane_head = lax.broadcasted_iota(jnp.int32, (wtok, LANES), 1) // HDIM

    def pump(step):
        moves = {
            1: lambda: links.to_third(1, 0),
            3: lambda: links.to_second(2, 0),
            wins - 1 + wins: lambda: links.to_second(3, 0),
            wins + wins: lambda: links.to_third(2, 0),
            3 * wins: lambda: links.to_third(3, 0),
        }
        for at, move in moves.items():
            pl.when(step == at)(move)

    def out_piece(slot):
        b, w = order[slot]
        for l in range(levels):
            for r in range(WLAT):
                t = pl.ds(slot * wtok + (l * WLAT + r) * WLON, WLON)
                grid_s[l, SH + b * WLAT + r, pl.ds(SL + w * WLON, WLON), :] = tok_s[t, :]

    def narrow(rows, cols):
        def row(r, _):
            for l in range(levels):
                ext_s[l, r, cols, :] = grid_s[l, r, cols, :].astype(jnp.bfloat16)
            return 0

        lax.fori_loop(rows[0], rows[1], row, 0)

    lat_next, lon_next, following = links.device(lat=1), links.device(lon=1), links.device(lat=1, lon=1)
    lower = pl.ds(SH, clat - SH)
    back = [
        links.copy("back_rows", ext_s.at[:, below, body_cols], resid_ref.at[:, top], lat_next),
        links.copy("back_cols", ext_s.at[:, lower, beyond], cols_ref.at[:, lower], lon_next),
        links.copy("back_corner", ext_s.at[:, below, beyond], cols_ref.at[:, top], following),
    ]

    def group(g, _):
        base = pl.multiple_of(g * gtok, gtok)
        mine = pl.ds(base, gtok)
        for part in range(3):
            at = pl.ds(part * width, width)
            qkv_s[:, at] = dot32(normed_s[mine, :], wqkv[part * width : (part + 1) * width], NT).astype(jnp.bfloat16)

        def window(w, _):
            pump(g * wins + w)
            rows = pl.ds(pl.multiple_of(w * wtok, wtok), wtok)
            hot = hot_s[pl.ds(pl.multiple_of(base + w * wtok, wtok), wtok), :].astype(jnp.bfloat16)
            barred = ((hot.astype(jnp.float32) - 1.0) * BIG).astype(jnp.bfloat16)
            for h4 in range(width // LANES):
                q = qkv_s[rows, pl.ds(h4 * LANES, LANES)]
                k = qkv_s[rows, pl.ds(width + h4 * LANES, LANES)]
                v = qkv_s[rows, pl.ds(2 * width + h4 * LANES, LANES)]
                queries = jnp.concatenate(
                    [
                        jnp.concatenate([jnp.where(lane_head == h, q, jnp.zeros_like(q)), hot], axis=1)
                        for h in range(per)
                    ],
                    axis=0,
                )
                keys = jnp.concatenate([k, barred], axis=1)
                scores = dot32(keys, queries, NT)
                most = jnp.max(scores, axis=0, keepdims=True)
                probs = jnp.exp2((scores - most) * EXP2_SCALE)
                total = jnp.sum(probs, axis=0, keepdims=True)
                mixed = dot32(v, probs.astype(jnp.bfloat16), TN) * (1.0 / total)
                heads = [mixed[h * HDIM : (h + 1) * HDIM, h * wtok : (h + 1) * wtok] for h in range(per)]
                mix_s[rows, pl.ds(h4 * LANES, LANES)] = jnp.concatenate(heads, axis=0).T.astype(jnp.bfloat16)
            return 0

        lax.fori_loop(0, wins, window, 0)

        @pl.when(g == 0)
        def _():
            links.to_cross(1, 0)
            links.arrive(1)

        wproj = wproj_s[...].reshape(width, width)
        attn_out = dot32(mix_s[...], wproj, NT).astype(jnp.bfloat16).astype(jnp.float32)
        tok_s[mine, :] += attn_out

        @pl.when(g == (late - 1) // wins)
        def _():
            for slot in range(early, late):
                out_piece(slot)
            narrow((clat, clat + SH), pl.ds(0, clon + PAD))
            narrow((SH, clat), pl.ds(clon, PAD))
            for copy in back:
                copy.start()

        return 0

    lax.fori_loop(0, groups, group, 0)
    for slot in list(range(early)) + list(range(late, count)):
        out_piece(slot)
    narrow((SH, clat), pl.ds(0, clon))
    keep = pltpu.make_async_copy(ext_s.at[:, lower, body_cols], resid_ref.at[:, lower], own_sem.at[0])
    keep.start()
    for i in (2, 3):
        links.to_cross(i, 0)
    for copy in rows_in + cols_in:
        copy.wait_send()
    for i in (0, 1):
        links.drain(i)
    for i in (2, 3):
        links.arrive(i)
        links.drain(i)
    for copy in back:
        copy.wait()
    keep.wait()


def attention(member, hot, gain, shards):
    dims = {"mem": lax.axis_size("mem") // 2, "lat": lax.axis_size("lat"), "lon": lax.axis_size("lon")}
    lead = (dims["mem"], 2, dims["lat"], dims["lon"])
    levels, clat, clon, width = member.shape
    bands, wins = clat // WLAT, clon // WLON
    ntok = levels * clat * clon
    gtok = ntok // bands
    slots = len(gather_keys(dims)) + len(HALO)
    anywhere = pl.BlockSpec(memory_space=pl.ANY)
    ext = (levels, clat + SH, clon + PAD, width)
    hot_ext = (clat + SH, clon + PAD, LANES)
    whole = [lead + s.shape for s in shards]
    outs = pl.pallas_call(
        functools.partial(attention_kernel, dims),
        out_shape=[
            jax.ShapeDtypeStruct(member.shape, jnp.bfloat16),
            jax.ShapeDtypeStruct((levels, clat, PAD, width), jnp.bfloat16),
            jax.ShapeDtypeStruct(whole[2], jnp.bfloat16),
            jax.ShapeDtypeStruct(whole[3], jnp.bfloat16),
        ],
        in_specs=[anywhere, anywhere, pl.BlockSpec(memory_space=pltpu.VMEM)] + [anywhere] * 4,
        out_specs=[anywhere] * 4,
        scratch_shapes=[
            pltpu.VMEM(ext, jnp.bfloat16),
            pltpu.VMEM(hot_ext, jnp.bfloat16),
            pltpu.VMEM(ext, jnp.float32),
            pltpu.VMEM(hot_ext, jnp.float32),
            pltpu.VMEM((ntok, width), jnp.float32),
            pltpu.VMEM((ntok, LANES), jnp.float32),
            pltpu.VMEM((ntok, width), jnp.bfloat16),
            pltpu.VMEM((gtok, 3 * width), jnp.bfloat16),
            pltpu.VMEM((gtok, width), jnp.bfloat16),
            pltpu.VMEM(whole[0], jnp.bfloat16),
            pltpu.VMEM(whole[1], jnp.bfloat16),
            pltpu.SemaphoreType.DMA((6,)),
            pltpu.SemaphoreType.DMA((slots,)),
            pltpu.SemaphoreType.DMA((slots,)),
        ],
        compiler_params=pltpu.CompilerParams(
            collective_id=0, has_side_effects=True, vmem_limit_bytes=56 * 2**20
        ),
        cost_estimate=pl.CostEstimate(
            flops=8 * ntok * width * width, bytes_accessed=4 * ntok * width, transcendentals=ntok * 4096
        ),
    )(member, hot, gain, *shards)
    return outs[0], outs[1], outs[2].reshape(-1, width), outs[3].reshape(width, -1)


def mlp_kernel(resid_ref, cols_ref, gain_ref, wup_ref, wdown_ref, out_ref, acc_s):
    levels, rows, cols, width = out_ref.shape
    hidden_all = wup_ref.shape[0]
    block = resid_ref[...].astype(jnp.float32)
    came = cols_ref[...].astype(jnp.float32)
    ours = lax.broadcasted_iota(jnp.int32, came.shape, 2) >= SL
    edge = jnp.where(ours, block[:, :, :PAD], came)
    resid = jnp.concatenate([edge, block[:, :, PAD:]], axis=2).reshape(levels * rows * cols, width)
    normed = norm(resid, gain_ref[...])
    acc_s[...] = resid
    step = min(width, hidden_all)
    for at in range(0, hidden_all, step):
        pre = dot32(normed, wup_ref[pl.ds(at, step), :], NT)
        hidden = (0.5 * pre * (1.0 + lax.erf(pre * 0.5**0.5))).astype(jnp.bfloat16)
        acc_s[...] += dot32(hidden, wdown_ref[:, pl.ds(at, step)], NT)
    out_ref[...] = acc_s[...].reshape(out_ref.shape).astype(jnp.bfloat16)


def whole(shape):
    return pl.BlockSpec(shape, lambda b: (0,) * len(shape))


def body(fields, region, gain_attn, w_qkv, w_proj, gain_mlp, w_up, w_down):
    member = fields[0]
    levels, clat, clon, width = member.shape
    bands = clat // WLAT
    count = levels * clat * clon

    north = (lax.axis_index("lat") * clat + jnp.arange(clat, dtype=jnp.int32)) < SH
    ids = region.astype(jnp.int32) + 3 * north[:, None].astype(jnp.int32)
    hot = (ids[:, :, None] == jnp.arange(LANES, dtype=jnp.int32)).astype(jnp.bfloat16)

    resid, came, wup_t, wdown_t = attention(
        member, hot, gain_attn[None], [w_qkv.T, w_proj.T, w_up.T, w_down.T]
    )

    grid_block = pl.BlockSpec((levels, WLAT, clon, width), lambda b: (0, b, 0, 0))
    came_block = pl.BlockSpec((levels, WLAT, PAD, width), lambda b: (0, b, 0, 0))
    out = pl.pallas_call(
        mlp_kernel,
        grid=(bands,),
        in_specs=[grid_block, came_block, whole((1, width)), whole(wup_t.shape), whole(wdown_t.shape)],
        out_specs=grid_block,
        out_shape=jax.ShapeDtypeStruct(member.shape, jnp.bfloat16),
        scratch_shapes=[pltpu.VMEM((count // bands, width), jnp.float32)],
        compiler_params=pltpu.CompilerParams(dimension_semantics=("arbitrary",), vmem_limit_bytes=56 * 2**20),
        cost_estimate=pl.CostEstimate(
            flops=4 * count * width * wup_t.shape[0], bytes_accessed=4 * count * width, transcendentals=count * 2048
        ),
    )(resid, came, gain_mlp[None], wup_t, wdown_t)
    return out[None]


def solution(mesh):
    columns = P(None, AXES)
    in_specs = (P("mem", None, "lat", "lon", None), P("lat", "lon"), P(), columns, columns, P(), columns, columns)
    out_specs = P("mem", None, "lat", "lon", None)
    return jax.shard_map(body, mesh=mesh, in_specs=in_specs, out_specs=out_specs, check_vma=False)
```

profile of v0, /device:TPU:11, one launch (start us, length us, event | category | flops | bytes accessed | tf_op | source)
XLA Modules:
  0.0 97.8 jit_solution(10224899069928259250)
XLA Ops:
  0.0 0.8 broadcast_add_fusion
  0.8 0.9 fusion.hot_ref
  1.7 80.8 %shard_map.82 = (bf16[2,24,48,512]{3,2,1,0:T(8,128)(2,1)}, bf16[2,24,8,512]{3,2,1,0:T(8,128)(2,1)}, bf16[2,2,4,2,64,512]{5,4,3,2,1,0:T(8,128)(2,1)}, bf16[2,2,4,2,16,2048]{5,4,3,2,1,0:T(8,128)(2,1)}) custom-call(bf16[2,24,48,512]{3,2,1,0:T(8,128)(2,1)} %bitcast.10, bf16[24,48,128]{2,1,0:T(8,128)(2,1)} %fusion.hot_ref, f32[1,512]{1,0:T(1,128)} %bitcast.15, ...), custom_call_target="tpu_custom_call" | custom-call | flops 4831838208 | bytes 4718592 | tf_op jit(solution)/shard_map/pallas_call | solution.py:445
  82.5 15.3 %shard_map.83 = bf16[2,24,48,512]{3,2,1,0:T(8,128)(2,1)} custom-call(bf16[2,24,48,512]{3,2,1,0:T(8,128)(2,1)} %get-tuple-element.9.resid_ref, bf16[2,24,8,512]{3,2,1,0:T(8,128)(2,1)} %get-tuple-element.10.cols_ref, f32[1,512]{1,0:T(1,128)} %bitcast.16, bf16[2048,512]{1,0:T(8,128)(2,1)} %bitcast.17, bf16[512,2048]{1,0:T(8,128)(2,1)} %bitcast.18), custom_call_target="tpu_custom_call" | custom-call | flops 9663676416 | bytes 4718592 | tf_op jit(solution)/shard_map/pallas_call | solution.py:519
  (1 shorter events, 0.0 us)
where the time goes:
time: 98.1 us; the launch traced here: 97.8 us
  Pallas kernels  96.1 us (98%)
  other arithmetic  1.72 us (2%)
    pallas_call x1, Pallas kernels, attention(): pl.pallas_call(functools.partial(attention_kernel, dims), out_shape=[jax....  80.8 us
    pallas_call x1, Pallas kernels, body(): pl.pallas_call(mlp_kernel, grid=(bands,), in_specs=[grid_block, came_bloc...  15.3 us

commit v1 on v0

--- a/solution.py
+++ b/solution.py
@@ -37,15 +37,25 @@
 
 
 def window_order(bands, wins):
-    edge = [(bands - 1, w) for w in range(wins)] + [(b, wins - 1) for b in range(bands - 1)]
+    rows = [(bands - 1, w) for w in range(wins - 1)]
+    cols = [(b, wins - 1) for b in range(bands)]
     inner = [(b, w) for b in range(bands - 1) for w in range(wins - 1)]
-    order = inner[:wins] + edge
-    return order + inner[wins:], wins, len(order)
+    order, inner = inner[:wins], inner[wins:]
+    marks = []
+    for edge in (rows, cols):
+        fill = -len(edge) % wins
+        marks.append((len(order), len(order) + len(edge)))
+        order, inner = order + edge + inner[:fill], inner[fill:]
+    return order + inner, marks[0], marks[1]
 
 
 def gather_plan(dims):
-    fine = [(d, "lon", "mem") if d % 2 == 0 else (d, "mem", "lon") for d in range(dims["lat"])]
-    return [fine, [(None, "lon", "mem")], [(None, "lon", "mem")], [(None, "lon", "mem")]]
+    last, middle = dims["lat"] - 1, dims["lat"] // 2
+    ways = ("lon", "mem"), ("mem", "lon")
+    fine = [(d,) + ways[d == last] for d in range(dims["lat"])]
+    up = [(d,) + ways[d == middle] for d in range(dims["lat"])]
+    down = [(d,) + ways[0] for d in range(dims["lat"])]
+    return [fine, [(None,) + ways[0]], up, down]
 
 
 def gather_keys(dims):
@@ -60,6 +70,7 @@
 
 
 HALO = ("rows", "cols", "corner", "id_rows", "id_cols", "id_corner", "back_rows", "back_cols", "back_corner")
+STAGES = 4
 
 
 class Links:
@@ -132,8 +143,12 @@
         return range(1, self.dims[axis])
 
     def start_first(self, i):
-        for d in self.peers("lat"):
+        for d in self.near():
             self.first(i, d).start()
+
+    def near(self):
+        n = self.dims["lat"]
+        return sorted(self.peers("lat"), key=lambda d: min(d, n - d))
 
     def to_second(self, i, p):
         lat, a2, _ = self.plan[i][p]
@@ -196,7 +211,7 @@
 def attention_kernel(
     dims,
     x_ref,
-    hot_ref,
+    region_ref,
     gain_ref,
     wqkv_ref,
     wproj_ref,
@@ -207,7 +222,7 @@
     up_ref,
     down_ref,
     ext_s,
-    hotx_s,
+    ids_s,
     grid_s,
     hotg_s,
     tok_s,
@@ -215,6 +230,8 @@
     normed_s,
     qkv_s,
     mix_s,
+    score_s,
+    prob_s,
     wqkv_s,
     wproj_s,
     own_sem,
@@ -224,10 +241,12 @@
     levels, clat, clon, width = x_ref.shape
     bands, wins = clat // WLAT, clon // WLON
     wtok = levels * WLAT * WLON
-    order, early, late = window_order(bands, wins)
+    order, (row_first, row_last), (col_first, col_last) = window_order(bands, wins)
     count = len(order)
     groups = count // wins
     gtok = wins * wtok
+    chunks = dims["lat"]
+    edge = list(range(row_first, row_last)) + list(range(col_first, col_last))
 
     links = Links(dims, [wqkv_s, wproj_s, up_ref, down_ref], send_sem, recv_sem)
     own = [
@@ -235,45 +254,52 @@
         for i, shard in enumerate([wqkv_ref, wproj_ref, wup_ref, wdown_ref])
     ]
     own.append(pltpu.make_async_copy(x_ref, ext_s.at[:, pl.ds(0, clat), pl.ds(0, clon)], own_sem.at[4]))
-    own.append(pltpu.make_async_copy(hot_ref, hotx_s.at[pl.ds(0, clat), pl.ds(0, clon)], own_sem.at[5]))
     for copy in own:
         copy.start()
+
+    north = lax.broadcasted_iota(jnp.int32, (clat, clon), 0) + lax.axis_index("lat") * clat < SH
+    ids_s[0] = jnp.zeros((clat, LANES), jnp.float32)
+    ids_s[0, :, pl.ds(0, clon)] = (region_ref[...] + jnp.where(north, 3, 0)).astype(jnp.float32)
 
     top, side = pl.ds(0, SH), pl.ds(0, PAD)
     body_rows, body_cols = pl.ds(0, clat), pl.ds(0, clon)
     below, beyond = pl.ds(clat, SH), pl.ds(clon, PAD)
     lat_prev, lon_prev, prev = links.device(lat=-1), links.device(lon=-1), links.device(lat=-1, lon=-1)
-    rows_in = [
-        links.copy("rows", x_ref.at[:, top], ext_s.at[:, below, body_cols], lat_prev),
-        links.copy("id_rows", hot_ref.at[top], hotx_s.at[below, body_cols], lat_prev),
+    ids_in = [
+        links.copy("id_rows", ids_s.at[0], ids_s.at[1], lat_prev),
+        links.copy("id_cols", ids_s.at[0], ids_s.at[2], lon_prev),
+        links.copy("id_corner", ids_s.at[0], ids_s.at[3], prev),
     ]
+    rows_in = [links.copy("rows", x_ref.at[:, top], ext_s.at[:, below, body_cols], lat_prev)]
     cols_in = [
         links.copy("cols", x_ref.at[:, :, side], ext_s.at[:, body_rows, beyond], lon_prev),
-        links.copy("id_cols", hot_ref.at[:, side], hotx_s.at[body_rows, beyond], lon_prev),
         links.copy("corner", x_ref.at[:, top, side], ext_s.at[:, below, beyond], prev),
-        links.copy("id_corner", hot_ref.at[top, side], hotx_s.at[below, beyond], prev),
     ]
 
     links.greet()
     own[0].wait()
     links.start_first(0)
     links.to_second(0, 0)
-    for copy in rows_in:
-        copy.start()
-    for i in range(1, 4):
-        own[i].wait()
-        links.start_first(i)
-    for copy in own[4:]:
+    for copy in own[1:]:
         copy.wait()
 
     def widen(rows, cols):
         def row(r, _):
             for l in range(levels):
                 grid_s[l, r, cols, :] = ext_s[l, r, cols, :].astype(jnp.float32)
-            hotg_s[r, cols, :] = hotx_s[r, cols, :].astype(jnp.float32)
             return 0
 
         lax.fori_loop(rows[0], rows[1], row, 0)
+
+    def one_hot(planes, rows, cols):
+        turned = planes.T
+        lane = lax.broadcasted_iota(jnp.int32, (cols, LANES), 1).astype(jnp.float32)
+        for r in range(rows[1] - rows[0]):
+            hotg_s[rows[0] + r, pl.ds(0, cols), :] = jnp.where(turned[:cols, r : r + 1] == lane, 1.0, 0.0)
+
+    def joined(here, there):
+        lane = lax.broadcasted_iota(jnp.int32, here.shape, 1)
+        return jnp.where(lane < clon, here, pltpu.roll(there, clon, 1))
 
     def fetch(slot):
         b, w = order[slot]
@@ -292,45 +318,94 @@
 
         lax.fori_loop(first, last, one, 0)
 
-    fine = len(links.plan[0])
+    near = links.near()
+    half = wins // 2
     widen((0, clat), pl.ds(0, clon))
-    for p in range(1, fine):
+    links.to_second(0, near[0])
+    links.to_third(0, 0)
+    links.start_first(1)
+    one_hot(ids_s[0], (0, clat), clon)
+    for slot in range(half):
+        fetch(slot)
+    for p in near[1:]:
         links.to_second(0, p)
-    links.to_third(0, 0)
-    for copy in cols_in:
+    links.start_first(2)
+    links.to_second(2, 0)
+    for slot in range(half, wins):
+        fetch(slot)
+    for p in near:
+        links.to_third(0, p)
+    for copy in rows_in + ids_in:
         copy.start()
-    for slot in list(range(early)) + list(range(late, count)):
-        fetch(slot)
-    for p in range(1, fine):
-        links.to_third(0, p)
-    norms(0, early)
-    norms(late, count)
-    for p in range(fine):
+    links.start_first(3)
+    links.to_second(1, 0)
+    links.to_third(2, 0)
+    norms(0, wins)
+    for slot in range(row_last, count):
+        if slot not in edge:
+            fetch(slot)
+    norms(row_last, col_first)
+    norms(col_last, count)
+    for p in [0] + near:
         links.to_cross(0, p)
-    links.to_second(1, 0)
-    for copy in rows_in + cols_in:
-        copy.wait_recv()
-    widen((0, clat), pl.ds(clon, PAD))
-    widen((clat, clat + SH), pl.ds(0, clon + PAD))
-    for slot in range(early, late):
-        fetch(slot)
-    norms(early, late)
+    links.to_second(3, 0)
+    links.to_second(2, near[0])
     links.arrive(0)
+
+    def fetch_rows():
+        for copy in ids_in + rows_in:
+            copy.wait_recv()
+        widen((clat, clat + SH), pl.ds(0, clon))
+        one_hot(joined(ids_s[0], ids_s[2]), (0, clat), clon + PAD)
+        one_hot(joined(ids_s[1, :PAD], ids_s[3, :PAD]), (clat, clat + SH), clon + PAD)
+        for slot in range(row_first, row_last):
+            fetch(slot)
+        norms(row_first, row_last)
+
+    def fetch_cols():
+        for copy in cols_in:
+            copy.wait_recv()
+        widen((0, clat + SH), pl.ds(clon, PAD))
+        for slot in range(col_first, col_last):
+            fetch(slot)
+        norms(col_first, col_last)
 
     wqkv = wqkv_s[...].reshape(3 * width, width)
     per = LANES // HDIM
+    fours = width // LANES
+    per_step = 2 if wins % 2 == 0 else 1
     lane_head = lax.broadcasted_iota(jnp.int32, (wtok, LANES), 1) // HDIM
 
+    moves = {}
+
+    def at_step(step, *move):
+        moves.setdefault(step, []).append(move)
+
+    def start_cols():
+        for copy in cols_in:
+            copy.start()
+
+    at_step(0, start_cols)
+    at_step(0, links.to_third, 1, 0)
+    for n, p in enumerate(near[1:]):
+        at_step(2 * n + 1, links.to_second, 2, p)
+    for n, p in enumerate(near):
+        at_step(3 + n, links.to_third, 2, p)
+    for n, p in enumerate(near):
+        at_step(3 + n, links.to_second, 3, p)
+    at_step(4, links.to_third, 3, 0)
+    for n, p in enumerate(near):
+        at_step(5 + n, links.to_third, 3, p)
+    for p in range(chunks):
+        at_step(7, links.to_cross, 2, p)
+
     def pump(step):
-        moves = {
-            1: lambda: links.to_third(1, 0),
-            3: lambda: links.to_second(2, 0),
-            wins - 1 + wins: lambda: links.to_second(3, 0),
-            wins + wins: lambda: links.to_third(2, 0),
-            3 * wins: lambda: links.to_third(3, 0),
-        }
-        for at, move in moves.items():
-            pl.when(step == at)(move)
+        for at, todo in moves.items():
+
+            @pl.when(step == at)
+            def _():
+                for move, *where in todo:
+                    move(*where)
 
     def out_piece(slot):
         b, w = order[slot]
@@ -358,37 +433,56 @@
     def group(g, _):
         base = pl.multiple_of(g * gtok, gtok)
         mine = pl.ds(base, gtok)
+        pl.when(g == row_first // wins)(fetch_rows)
+        pl.when(g == col_first // wins)(fetch_cols)
         for part in range(3):
             at = pl.ds(part * width, width)
             qkv_s[:, at] = dot32(normed_s[mine, :], wqkv[part * width : (part + 1) * width], NT).astype(jnp.bfloat16)
 
-        def window(w, _):
-            pump(g * wins + w)
-            rows = pl.ds(pl.multiple_of(w * wtok, wtok), wtok)
-            hot = hot_s[pl.ds(pl.multiple_of(base + w * wtok, wtok), wtok), :].astype(jnp.bfloat16)
-            barred = ((hot.astype(jnp.float32) - 1.0) * BIG).astype(jnp.bfloat16)
-            for h4 in range(width // LANES):
-                q = qkv_s[rows, pl.ds(h4 * LANES, LANES)]
-                k = qkv_s[rows, pl.ds(width + h4 * LANES, LANES)]
-                v = qkv_s[rows, pl.ds(2 * width + h4 * LANES, LANES)]
-                queries = jnp.concatenate(
-                    [
-                        jnp.concatenate([jnp.where(lane_head == h, q, jnp.zeros_like(q)), hot], axis=1)
-                        for h in range(per)
-                    ],
-                    axis=0,
-                )
-                keys = jnp.concatenate([k, barred], axis=1)
-                scores = dot32(keys, queries, NT)
+        def windows(u, _):
+            pump(g * (wins // per_step) + u)
+            rows = [pl.ds(pl.multiple_of((u * per_step + j) * wtok, wtok), wtok) for j in range(per_step)]
+            hots = []
+            for j in range(per_step):
+                at = pl.multiple_of(base + (u * per_step + j) * wtok, wtok)
+                hot = hot_s[pl.ds(at, wtok), :].astype(jnp.bfloat16)
+                hots.append((hot, ((hot.astype(jnp.float32) - 1.0) * BIG).astype(jnp.bfloat16)))
+
+            def score(i):
+                j, f = divmod(i, fours)
+                hot, barred = hots[j]
+                q = qkv_s[rows[j], pl.ds(f * LANES, LANES)]
+                k = qkv_s[rows[j], pl.ds(width + f * LANES, LANES)]
+                queries = [jnp.concatenate([jnp.where(lane_head == h, q, jnp.zeros_like(q)), hot], axis=1) for h in range(per)]
+                score_s[i % STAGES] = dot32(jnp.concatenate([k, barred], axis=1), jnp.concatenate(queries, axis=0), NT)
+
+            def soften(i):
+                scores = score_s[i % STAGES]
                 most = jnp.max(scores, axis=0, keepdims=True)
-                probs = jnp.exp2((scores - most) * EXP2_SCALE)
-                total = jnp.sum(probs, axis=0, keepdims=True)
-                mixed = dot32(v, probs.astype(jnp.bfloat16), TN) * (1.0 / total)
-                heads = [mixed[h * HDIM : (h + 1) * HDIM, h * wtok : (h + 1) * wtok] for h in range(per)]
-                mix_s[rows, pl.ds(h4 * LANES, LANES)] = jnp.concatenate(heads, axis=0).T.astype(jnp.bfloat16)
+                prob_s[i % STAGES] = jnp.exp2((scores - most) * EXP2_SCALE).astype(jnp.bfloat16)
+
+            def mix(i):
+                j, f = divmod(i, fours)
+                v = qkv_s[rows[j], pl.ds(2 * width + f * LANES, LANES)]
+                ones = jnp.ones((wtok, HDIM // 2), jnp.bfloat16)
+                mixed = dot32(jnp.concatenate([v, ones], axis=1), prob_s[i % STAGES], TN)
+                heads = []
+                for h in range(per):
+                    at = slice(h * wtok, (h + 1) * wtok)
+                    heads.append(mixed[h * HDIM : (h + 1) * HDIM, at] * (1.0 / mixed[LANES : LANES + 1, at]))
+                mix_s[rows[j], pl.ds(f * LANES, LANES)] = jnp.concatenate(heads, axis=0).astype(jnp.bfloat16).T
+
+            items = per_step * fours
+            for t in range(items + 3):
+                if t < items:
+                    score(t)
+                if 0 <= t - 2 < items:
+                    soften(t - 2)
+                if 0 <= t - 3 < items:
+                    mix(t - 3)
             return 0
 
-        lax.fori_loop(0, wins, window, 0)
+        lax.fori_loop(0, wins // per_step, windows, 0)
 
         @pl.when(g == 0)
         def _():
@@ -399,9 +493,9 @@
         attn_out = dot32(mix_s[...], wproj, NT).astype(jnp.bfloat16).astype(jnp.float32)
         tok_s[mine, :] += attn_out
 
-        @pl.when(g == (late - 1) // wins)
+        @pl.when(g == (col_last - 1) // wins)
         def _():
-            for slot in range(early, late):
+            for slot in edge:
                 out_piece(slot)
             narrow((clat, clat + SH), pl.ds(0, clon + PAD))
             narrow((SH, clat), pl.ds(clon, PAD))
@@ -411,14 +505,15 @@
         return 0
 
     lax.fori_loop(0, groups, group, 0)
-    for slot in list(range(early)) + list(range(late, count)):
-        out_piece(slot)
+    for slot in range(count):
+        if slot not in edge:
+            out_piece(slot)
     narrow((SH, clat), pl.ds(0, clon))
     keep = pltpu.make_async_copy(ext_s.at[:, lower, body_cols], resid_ref.at[:, lower], own_sem.at[0])
     keep.start()
-    for i in (2, 3):
-        links.to_cross(i, 0)
-    for copy in rows_in + cols_in:
+    for p in range(chunks):
+        links.to_cross(3, p)
+    for copy in ids_in + rows_in + cols_in:
         copy.wait_send()
     for i in (0, 1):
         links.drain(i)
@@ -430,7 +525,7 @@
     keep.wait()
 
 
-def attention(member, hot, gain, shards):
+def attention(member, region, gain, shards):
     dims = {"mem": lax.axis_size("mem") // 2, "lat": lax.axis_size("lat"), "lon": lax.axis_size("lon")}
     lead = (dims["mem"], 2, dims["lat"], dims["lon"])
     levels, clat, clon, width = member.shape
@@ -450,11 +545,11 @@
             jax.ShapeDtypeStruct(whole[2], jnp.bfloat16),
             jax.ShapeDtypeStruct(whole[3], jnp.bfloat16),
         ],
-        in_specs=[anywhere, anywhere, pl.BlockSpec(memory_space=pltpu.VMEM)] + [anywhere] * 4,
+        in_specs=[anywhere] + [pl.BlockSpec(memory_space=pltpu.VMEM)] * 2 + [anywhere] * 4,
         out_specs=[anywhere] * 4,
         scratch_shapes=[
             pltpu.VMEM(ext, jnp.bfloat16),
-            pltpu.VMEM(hot_ext, jnp.bfloat16),
+            pltpu.VMEM((4, clat, LANES), jnp.float32),
             pltpu.VMEM(ext, jnp.float32),
             pltpu.VMEM(hot_ext, jnp.float32),
             pltpu.VMEM((ntok, width), jnp.float32),
@@ -462,9 +557,11 @@
             pltpu.VMEM((ntok, width), jnp.bfloat16),
             pltpu.VMEM((gtok, 3 * width), jnp.bfloat16),
             pltpu.VMEM((gtok, width), jnp.bfloat16),
+            pltpu.VMEM((STAGES, gtok // wins, (LANES // HDIM) * gtok // wins), jnp.float32),
+            pltpu.VMEM((STAGES, gtok // wins, (LANES // HDIM) * gtok // wins), jnp.bfloat16),
             pltpu.VMEM(whole[0], jnp.bfloat16),
             pltpu.VMEM(whole[1], jnp.bfloat16),
-            pltpu.SemaphoreType.DMA((6,)),
+            pltpu.SemaphoreType.DMA((5,)),
             pltpu.SemaphoreType.DMA((slots,)),
             pltpu.SemaphoreType.DMA((slots,)),
         ],
@@ -474,7 +571,7 @@
         cost_estimate=pl.CostEstimate(
             flops=8 * ntok * width * width, bytes_accessed=4 * ntok * width, transcendentals=ntok * 4096
         ),
-    )(member, hot, gain, *shards)
+    )(member, region, gain, *shards)
     return outs[0], outs[1], outs[2].reshape(-1, width), outs[3].reshape(width, -1)
 
 
@@ -506,12 +603,8 @@
     bands = clat // WLAT
     count = levels * clat * clon
 
-    north = (lax.axis_index("lat") * clat + jnp.arange(clat, dtype=jnp.int32)) < SH
-    ids = region.astype(jnp.int32) + 3 * north[:, None].astype(jnp.int32)
-    hot = (ids[:, :, None] == jnp.arange(LANES, dtype=jnp.int32)).astype(jnp.bfloat16)
-
     resid, came, wup_t, wdown_t = attention(
-        member, hot, gain_attn[None], [w_qkv.T, w_proj.T, w_up.T, w_down.T]
+        member, region, gain_attn[None], [w_qkv.T, w_proj.T, w_up.T, w_down.T]
     )
 
     grid_block = pl.BlockSpec((levels, WLAT, clon, width), lambda b: (0, b, 0, 0))

time: 98.1 us -> 73.5 us (0.75)
  the two profiles are of different devices: /device:TPU:11 before, /device:TPU:19 now
where the time goes in v1:
time: 73.5 us; the launch traced here: 73.3 us
  Pallas kernels  73.2 us (100%)
    pallas_call x1, Pallas kernels, attention(): pl.pallas_call(functools.partial(attention_kernel, dims), out_shape=[jax....  57.9 us
    pallas_call x1, Pallas kernels, body(): pl.pallas_call(mlp_kernel, grid=(bands,), in_specs=[grid_block, came_bloc...  15.3 us

profile of v1, /device:TPU:19, one launch (start us, length us, event | category | flops | bytes accessed | tf_op | source)
XLA Modules:
  0.0 73.3 jit_solution(5526872816395003302)
XLA Ops:
  0.0 57.9 %shard_map.82 = (bf16[2,24,48,512]{3,2,1,0:T(8,128)(2,1)}, bf16[2,24,8,512]{3,2,1,0:T(8,128)(2,1)}, bf16[2,2,4,2,64,512]{5,4,3,2,1,0:T(8,128)(2,1)}, bf16[2,2,4,2,16,2048]{5,4,3,2,1,0:T(8,128)(2,1)}) custom-call(bf16[2,24,48,512]{3,2,1,0:T(8,128)(2,1)} %bitcast.10, s32[24,48]{1,0:T(8,128)} %region_ref.1, f32[1,512]{1,0:T(1,128)} %bitcast.15, ...), custom_call_target="tpu_custom_call" | custom-call | flops 4831838208 | bytes 4718592 | tf_op jit(solution)/shard_map/pallas_call | solution.py:540
  57.9 15.3 %shard_map.83 = bf16[2,24,48,512]{3,2,1,0:T(8,128)(2,1)} custom-call(bf16[2,24,48,512]{3,2,1,0:T(8,128)(2,1)} %get-tuple-element.9.resid_ref, bf16[2,24,8,512]{3,2,1,0:T(8,128)(2,1)} %get-tuple-element.10.cols_ref, f32[1,512]{1,0:T(1,128)} %bitcast.16, bf16[2048,512]{1,0:T(8,128)(2,1)} %bitcast.17, bf16[512,2048]{1,0:T(8,128)(2,1)} %bitcast.18), custom_call_target="tpu_custom_call" | custom-call | flops 9663676416 | bytes 4718592 | tf_op jit(solution)/shard_map/pallas_call | solution.py:612

commit v2 on v1

--- a/solution.py
+++ b/solution.py
@@ -52,10 +52,14 @@
 def gather_plan(dims):
     last, middle = dims["lat"] - 1, dims["lat"] // 2
     ways = ("lon", "mem"), ("mem", "lon")
-    fine = [(d,) + ways[d == last] for d in range(dims["lat"])]
+    fine = [(d, "all", None) for d in range(dims["lat"])]
     up = [(d,) + ways[d == middle] for d in range(dims["lat"])]
-    down = [(d,) + ways[0] for d in range(dims["lat"])]
+    down = [(d,) + ways[d == middle] for d in range(dims["lat"])]
     return [fine, [(None,) + ways[0]], up, down]
+
+
+def spread(dims):
+    return [(x, y) for x in range(dims["lon"] - 1, -1, -1) for y in range(dims["mem"] - 1, -1, -1) if x or y]
 
 
 def gather_keys(dims):
@@ -64,6 +68,9 @@
         keys += [("z", i, d) for d in range(1, dims["lat"])]
         for p, (_, a2, a3) in enumerate(parts):
             keys += [("c1", i, p)]
+            if a2 == "all":
+                keys += [(k, i, p, d) for d in spread(dims) for k in ("s2", "c2")]
+                continue
             keys += [(k, i, p, d) for d in range(1, dims[a2]) for k in ("s2", "c2")]
             keys += [(k, i, p, d) for d in range(1, dims[a3]) for k in ("s3", "c3")]
     return keys
@@ -121,7 +128,8 @@
 
     def second(self, i, p, d):
         block = self.block(i, lat=self.lat_of(i, p))
-        return self.copy(("s2", i, p, d), block, block, self.device(**{self.plan[i][p][1]: d}))
+        to = dict(zip(("lon", "mem"), d)) if isinstance(d, tuple) else {self.plan[i][p][1]: d}
+        return self.copy(("s2", i, p, d), block, block, self.device(**to))
 
     def third(self, i, p, d):
         block = self.block(i, lat=self.lat_of(i, p), **{self.plan[i][p][1]: ALL})
@@ -131,7 +139,8 @@
         _, a2, a3 = self.plan[i][p]
         where = {"lat": self.lat_of(i, p)}
         if stage == 2:
-            where[a2] = self.moved(a2, -d)
+            for axis, far in zip(("lon", "mem"), d) if a2 == "all" else [(a2, d)]:
+                where[axis] = self.moved(axis, -far)
         if stage == 3:
             where[a2] = ALL
             where[a3] = self.moved(a3, -d)
@@ -140,7 +149,9 @@
         return self.copy(key, block, block, self.partner)
 
     def peers(self, axis):
-        return range(1, self.dims[axis])
+        if axis is None:
+            return ()
+        return spread(self.dims) if axis == "all" else range(1, self.dims[axis])
 
     def start_first(self, i):
         for d in self.near():
@@ -202,6 +213,7 @@
         others = [self.partner]
         for axis in AXES:
             others += [self.device(**{axis: d}) for d in self.peers(axis)]
+        others += [self.device(lon=x, mem=y) for x, y in spread(self.dims) if x and y]
         others += [self.device(lat=1, lon=1), self.device(lat=-1, lon=-1)]
         for to in others:
             pl.semaphore_signal(barrier, inc=1, device_id=to, device_id_type=pl.DeviceIdType.MESH)
@@ -261,9 +273,9 @@
     ids_s[0] = jnp.zeros((clat, LANES), jnp.float32)
     ids_s[0, :, pl.ds(0, clon)] = (region_ref[...] + jnp.where(north, 3, 0)).astype(jnp.float32)
 
-    top, side = pl.ds(0, SH), pl.ds(0, PAD)
+    top, side = pl.ds(0, SH), pl.ds(0, SL)
     body_rows, body_cols = pl.ds(0, clat), pl.ds(0, clon)
-    below, beyond = pl.ds(clat, SH), pl.ds(clon, PAD)
+    below, beyond = pl.ds(clat, SH), pl.ds(clon, SL)
     lat_prev, lon_prev, prev = links.device(lat=-1), links.device(lon=-1), links.device(lat=-1, lon=-1)
     ids_in = [
         links.copy("id_rows", ids_s.at[0], ids_s.at[1], lat_prev),
@@ -348,6 +360,8 @@
     norms(col_last, count)
     for p in [0] + near:
         links.to_cross(0, p)
+    for copy in cols_in:
+        copy.start()
     links.to_second(3, 0)
     links.to_second(2, near[0])
     links.arrive(0)
@@ -373,7 +387,7 @@
     wqkv = wqkv_s[...].reshape(3 * width, width)
     per = LANES // HDIM
     fours = width // LANES
-    per_step = 2 if wins % 2 == 0 else 1
+    per_step = 4 if wins % 4 == 0 else 1
     lane_head = lax.broadcasted_iota(jnp.int32, (wtok, LANES), 1) // HDIM
 
     moves = {}
@@ -385,19 +399,18 @@
         for copy in cols_in:
             copy.start()
 
-    at_step(0, start_cols)
-    at_step(0, links.to_third, 1, 0)
+    at_step((0) // 2, links.to_third, 1, 0)
     for n, p in enumerate(near[1:]):
-        at_step(2 * n + 1, links.to_second, 2, p)
+        at_step(n, links.to_second, 2, p)
     for n, p in enumerate(near):
-        at_step(3 + n, links.to_third, 2, p)
+        at_step(1 + n // 2, links.to_third, 2, p)
     for n, p in enumerate(near):
-        at_step(3 + n, links.to_second, 3, p)
-    at_step(4, links.to_third, 3, 0)
+        at_step(1 + n // 2, links.to_second, 3, p)
+    at_step(1, links.to_third, 3, 0)
     for n, p in enumerate(near):
-        at_step(5 + n, links.to_third, 3, p)
+        at_step(2 + n // 2, links.to_third, 3, p)
     for p in range(chunks):
-        at_step(7, links.to_cross, 2, p)
+        at_step(3, links.to_cross, 2, p)
 
     def pump(step):
         for at, todo in moves.items():
@@ -426,8 +439,8 @@
     lower = pl.ds(SH, clat - SH)
     back = [
         links.copy("back_rows", ext_s.at[:, below, body_cols], resid_ref.at[:, top], lat_next),
-        links.copy("back_cols", ext_s.at[:, lower, beyond], cols_ref.at[:, lower], lon_next),
-        links.copy("back_corner", ext_s.at[:, below, beyond], cols_ref.at[:, top], following),
+        links.copy("back_cols", ext_s.at[:, lower, beyond], cols_ref.at[:, lower, pl.ds(0, SL)], lon_next),
+        links.copy("back_corner", ext_s.at[:, below, beyond], cols_ref.at[:, top, pl.ds(0, SL)], following),
     ]
 
     def group(g, _):
@@ -575,9 +588,8 @@
     return outs[0], outs[1], outs[2].reshape(-1, width), outs[3].reshape(width, -1)
 
 
-def mlp_kernel(resid_ref, cols_ref, gain_ref, wup_ref, wdown_ref, out_ref, acc_s):
+def mlp_kernel(resid_ref, cols_ref, gain_ref, wup_ref, wdown_ref, out_ref, acc_s, normed_s, hidden_s):
     levels, rows, cols, width = out_ref.shape
-    hidden_all = wup_ref.shape[0]
     block = resid_ref[...].astype(jnp.float32)
     came = cols_ref[...].astype(jnp.float32)
     ours = lax.broadcasted_iota(jnp.int32, came.shape, 2) >= SL
@@ -585,11 +597,15 @@
     resid = jnp.concatenate([edge, block[:, :, PAD:]], axis=2).reshape(levels * rows * cols, width)
     normed = norm(resid, gain_ref[...])
     acc_s[...] = resid
-    step = min(width, hidden_all)
-    for at in range(0, hidden_all, step):
-        pre = dot32(normed, wup_ref[pl.ds(at, step), :], NT)
-        hidden = (0.5 * pre * (1.0 + lax.erf(pre * 0.5**0.5))).astype(jnp.bfloat16)
-        acc_s[...] += dot32(hidden, wdown_ref[:, pl.ds(at, step)], NT)
+    tokens = levels * rows * cols
+    parts = 2 if tokens % 32 == 0 else 1
+    spans = [pl.ds(n * (tokens // parts), tokens // parts) for n in range(parts)]
+    normed_s[...] = normed
+    for span in spans:
+        pre = dot32(normed_s[span, :], wup_ref[...], NT)
+        hidden_s[span, :] = (0.5 * pre * (1.0 + lax.erf(pre * 0.5**0.5))).astype(jnp.bfloat16)
+    for span in spans:
+        acc_s[span, :] += dot32(hidden_s[span, :], wdown_ref[...], NT)
     out_ref[...] = acc_s[...].reshape(out_ref.shape).astype(jnp.bfloat16)
 
 
@@ -615,7 +631,11 @@
         in_specs=[grid_block, came_block, whole((1, width)), whole(wup_t.shape), whole(wdown_t.shape)],
         out_specs=grid_block,
         out_shape=jax.ShapeDtypeStruct(member.shape, jnp.bfloat16),
-        scratch_shapes=[pltpu.VMEM((count // bands, width), jnp.float32)],
+        scratch_shapes=[
+            pltpu.VMEM((count // bands, width), jnp.float32),
+            pltpu.VMEM((count // bands, width), jnp.bfloat16),
+            pltpu.VMEM((count // bands, wup_t.shape[0]), jnp.bfloat16),
+        ],
         compiler_params=pltpu.CompilerParams(dimension_semantics=("arbitrary",), vmem_limit_bytes=56 * 2**20),
         cost_estimate=pl.CostEstimate(
             flops=4 * count * width * wup_t.shape[0], bytes_accessed=4 * count * width, transcendentals=count * 2048

time: 73.5 us -> 70.6 us (0.961)
  the two profiles are of different devices: /device:TPU:19 before, /device:TPU:0 now
where the time goes in v2:
time: 70.6 us; the launch traced here: 70.4 us
  Pallas kernels  70.4 us (100%)
    pallas_call x1, Pallas kernels, attention(): pl.pallas_call(functools.partial(attention_kernel, dims), out_shape=[jax....  55.4 us
    pallas_call x1, Pallas kernels, body(): pl.pallas_call(mlp_kernel, grid=(bands,), in_specs=[grid_block, came_bloc...  15 us

profile of v2, /device:TPU:0, one launch (start us, length us, event | category | flops | bytes accessed | tf_op | source)
XLA Modules:
  0.0 70.4 jit_solution(16395211171901981688)
XLA Ops:
  0.0 55.4 %shard_map.82 = (bf16[2,24,48,512]{3,2,1,0:T(8,128)(2,1)}, bf16[2,24,8,512]{3,2,1,0:T(8,128)(2,1)}, bf16[2,2,4,2,64,512]{5,4,3,2,1,0:T(8,128)(2,1)}, bf16[2,2,4,2,16,2048]{5,4,3,2,1,0:T(8,128)(2,1)}) custom-call(bf16[2,24,48,512]{3,2,1,0:T(8,128)(2,1)} %bitcast.10, s32[24,48]{1,0:T(8,128)} %region_ref.1, f32[1,512]{1,0:T(1,128)} %bitcast.15, ...), custom_call_target="tpu_custom_call" | custom-call | flops 4831838208 | bytes 4718592 | tf_op jit(solution)/shard_map/pallas_call | solution.py:553
  55.4 15.0 %shard_map.83 = bf16[2,24,48,512]{3,2,1,0:T(8,128)(2,1)} custom-call(bf16[2,24,48,512]{3,2,1,0:T(8,128)(2,1)} %get-tuple-element.9.resid_ref, bf16[2,24,8,512]{3,2,1,0:T(8,128)(2,1)} %get-tuple-element.10.cols_ref, f32[1,512]{1,0:T(1,128)} %bitcast.16, bf16[2048,512]{1,0:T(8,128)(2,1)} %bitcast.17, bf16[512,2048]{1,0:T(8,128)(2,1)} %bitcast.18), custom_call_target="tpu_custom_call" | custom-call | flops 9663676416 | bytes 4718592 | tf_op jit(solution)/shard_map/pallas_call | solution.py:628

commit v3 on v2

--- a/solution.py
+++ b/solution.py
@@ -408,9 +408,7 @@
         at_step(1 + n // 2, links.to_second, 3, p)
     at_step(1, links.to_third, 3, 0)
     for n, p in enumerate(near):
-        at_step(2 + n // 2, links.to_third, 3, p)
-    for p in range(chunks):
-        at_step(3, links.to_cross, 2, p)
+        at_step(2 + (n > 0), links.to_third, 3, p)
 
     def pump(step):
         for at, todo in moves.items():
@@ -426,6 +424,15 @@
             for r in range(WLAT):
                 t = pl.ds(slot * wtok + (l * WLAT + r) * WLON, WLON)
                 grid_s[l, SH + b * WLAT + r, pl.ds(SL + w * WLON, WLON), :] = tok_s[t, :]
+
+    inner = [slot for slot in range(count) if slot not in edge]
+    ready = [slot for slot in inner if slot < col_first]
+
+    def out_ready():
+        for slot in ready:
+            out_piece(slot)
+
+    moves.setdefault(col_first // wins * (wins // per_step), []).insert(0, (out_ready,))
 
     def narrow(rows, cols):
         def row(r, _):
@@ -518,12 +525,14 @@
         return 0
 
     lax.fori_loop(0, groups, group, 0)
-    for slot in range(count):
-        if slot not in edge:
+    for slot in inner:
+        if slot not in ready:
             out_piece(slot)
     narrow((SH, clat), pl.ds(0, clon))
     keep = pltpu.make_async_copy(ext_s.at[:, lower, body_cols], resid_ref.at[:, lower], own_sem.at[0])
     keep.start()
+    for p in range(chunks):
+        links.to_cross(2, p)
     for p in range(chunks):
         links.to_cross(3, p)
     for copy in ids_in + rows_in + cols_in:

time: 70.6 us -> 70.9 us (level)
  no operation moved by 1% of the time
where the time goes in v3:
time: 70.9 us; the launch traced here: 70.6 us
  Pallas kernels  70.6 us (100%)
    pallas_call x1, Pallas kernels, attention(): pl.pallas_call(functools.partial(attention_kernel, dims), out_shape=[jax....  55.7 us
    pallas_call x1, Pallas kernels, body(): pl.pallas_call(mlp_kernel, grid=(bands,), in_specs=[grid_block, came_bloc...  15 us

profile of v3, /device:TPU:0, one launch (start us, length us, event | category | flops | bytes accessed | tf_op | source)
XLA Modules:
  0.0 70.6 jit_solution(10645509223858476196)
XLA Ops:
  0.0 55.7 %shard_map.82 = (bf16[2,24,48,512]{3,2,1,0:T(8,128)(2,1)}, bf16[2,24,8,512]{3,2,1,0:T(8,128)(2,1)}, bf16[2,2,4,2,64,512]{5,4,3,2,1,0:T(8,128)(2,1)}, bf16[2,2,4,2,16,2048]{5,4,3,2,1,0:T(8,128)(2,1)}) custom-call(bf16[2,24,48,512]{3,2,1,0:T(8,128)(2,1)} %bitcast.10, s32[24,48]{1,0:T(8,128)} %region_ref.1, f32[1,512]{1,0:T(1,128)} %bitcast.15, ...), custom_call_target="tpu_custom_call" | custom-call | flops 4831838208 | bytes 4718592 | tf_op jit(solution)/shard_map/pallas_call | solution.py:562
  55.7 15.0 %shard_map.83 = bf16[2,24,48,512]{3,2,1,0:T(8,128)(2,1)} custom-call(bf16[2,24,48,512]{3,2,1,0:T(8,128)(2,1)} %get-tuple-element.9.resid_ref, bf16[2,24,8,512]{3,2,1,0:T(8,128)(2,1)} %get-tuple-element.10.cols_ref, f32[1,512]{1,0:T(1,128)} %bitcast.16, bf16[2048,512]{1,0:T(8,128)(2,1)} %bitcast.17, bf16[512,2048]{1,0:T(8,128)(2,1)} %bitcast.18), custom_call_target="tpu_custom_call" | custom-call | flops 9663676416 | bytes 4718592 | tf_op jit(solution)/shard_map/pallas_call | solution.py:637
